TPU v7x, 256 devices: a whole 4x4x8 slice. The times are simulated.
256 devices in a mesh: shard: 32 (over z, x), width: 2 (over core), unit: 4 (over y).
Axes of the slice: x: 4, y: 4, z: 8, core: 2. Of those that a mesh axis runs over, the one named last changes fastest.
Arguments:
- w_gate: bfloat16 [14336, 14336], P(('unit', 'shard'), 'width'), parts along dimension 0, may hold values from -0.1875 to 0.1875
- low_gate: bfloat16 [14336, 64], P(('unit', 'shard')), parts along dimension 0, may hold values from -0.09375 to 0.09375
- high_gate: bfloat16 [256, 14336], P('unit', 'width'), parts along dimension 0, may hold values from -0.75 to 0.75
- w_up: bfloat16 [14336, 14336], P(('unit', 'shard'), 'width'), parts along dimension 0, may hold values from -0.1875 to 0.1875
- low_up: bfloat16 [14336, 64], P(('unit', 'shard')), parts along dimension 0, may hold values from -0.09375 to 0.09375
- high_up: bfloat16 [256, 14336], P('unit', 'width'), parts along dimension 0, may hold values from -0.75 to 0.75
- norm_train: float32 [14336], P(('unit', 'shard', 'width')), parts along dimension 0, may hold values from 0.25 to 1.75
- norm_step: float32 [14336], P(('unit', 'shard', 'width')), parts along dimension 0, may hold values from -0.3 to 0.3
Outputs:
- serve_gate: bfloat16 [14336, 14336], P('unit', ('width', 'shard')), parts along dimension 0
- serve_up: bfloat16 [14336, 14336], P('unit', ('width', 'shard')), parts along dimension 0
- column_gate: float32 [57344], P(('unit', 'width', 'shard')), parts along dimension 0
- column_up: float32 [57344], P(('unit', 'width', 'shard')), parts along dimension 0
- serve_norm: bfloat16 [14336], P('unit'), parts along dimension 0
There are 4 independent parts, one for each index of `unit`. A program takes and returns all parts, laid end to end along the dimension named above; each array names one. Nothing has to cross between parts.
All inputs are finite; a program needn't handle non-finite values. Where the computation divides by a largest or mean magnitude, that divisor is 1e-20 or more.
Results may differ from a plain program's by a relative error of at most 0.001.
Values may be sent and summed in bfloat16 or wider, within the bound.
A program may use at most 64 MiB of HBM per device.

v0:
```python
import jax
import jax.numpy as jnp
from jax import lax
from jax.sharding import Mesh
from jax.sharding import PartitionSpec as P

SHARD = ("shard_0", "shard_1")
SHARD_WIDTH = ("shard_0", "shard_1", "width")
UNIT_SHARD = ("unit", "shard_0", "shard_1")
UNIT_SHARD_WIDTH = ("unit", "shard_0", "shard_1", "width")
WIDTH_SHARD = ("width", "shard_0", "shard_1")
UNIT_WIDTH_SHARD = ("unit", "width", "shard_0", "shard_1")


mix_rate = 0.5


def one_axis_at_a_time(array, axes):
    for axis in axes:
        array = lax.pmax(array, axis)
    return array


def from_everyone(array, axis):
    count = lax.axis_size(axis)
    return lax.all_to_all(
        jnp.broadcast_to(array[None], (count, *array.shape)), axis, 0, 0, tiled=True
    )


def in_order(tiles, dim):
    dims = list(tiles.shape[1:])
    dims[dim] *= tiles.shape[0]
    return jnp.moveaxis(tiles, 0, dim).reshape(dims)


def collect(array, axis, dim):
    tiles = from_everyone(array, axis)
    return in_order(tiles, dim)


def local(w_gate, low_gate, high_gate, w_up, low_up, high_up, norm_train, norm_step):
    fresh_gate = w_gate.astype(jnp.float32) + mix_rate * jnp.dot(
        low_gate, high_gate, preferred_element_type=jnp.float32
    )
    fresh_up = w_up.astype(jnp.float32) + mix_rate * jnp.dot(
        low_up, high_up, preferred_element_type=jnp.float32
    )
    column_gate, column_up = (
        one_axis_at_a_time(jnp.max(jnp.abs(fresh_gate), axis=0), SHARD),
        one_axis_at_a_time(jnp.max(jnp.abs(fresh_up), axis=0), SHARD),
    )
    narrow_gate, narrow_up = (
        (fresh_gate / column_gate).astype(jnp.bfloat16),
        (fresh_up / column_up).astype(jnp.bfloat16),
    )
    serve_gate, serve_up = (
        lax.all_to_all(narrow_gate, SHARD, split_axis=1, concat_axis=0, tiled=True),
        lax.all_to_all(narrow_up, SHARD, split_axis=1, concat_axis=0, tiled=True),
    )
    place = lax.axis_index(SHARD)
    column_gate = lax.dynamic_slice_in_dim(
        column_gate, place * serve_gate.shape[1], serve_gate.shape[1]
    )
    column_up = lax.dynamic_slice_in_dim(column_up, place * serve_up.shape[1], serve_up.shape[1])
    serve_norm = collect((norm_train + norm_step).astype(jnp.bfloat16), SHARD_WIDTH, 0)
    return (serve_gate, serve_up, column_gate, column_up, serve_norm)


def solution(mesh):
    split = Mesh(
        mesh.devices.reshape(8, 4, mesh.shape["width"], mesh.shape["unit"]),
        ("shard_0", "shard_1", "width", "unit"),
    )
    return jax.shard_map(
        local,
        mesh=split,
        in_specs=(
            P(UNIT_SHARD, "width"),
            P(UNIT_SHARD, None),
            P("unit", "width"),
            P(UNIT_SHARD, "width"),
            P(UNIT_SHARD, None),
            P("unit", "width"),
            P(UNIT_SHARD_WIDTH),
            P(UNIT_SHARD_WIDTH),
        ),
        out_specs=(
            P("unit", WIDTH_SHARD),
            P("unit", WIDTH_SHARD),
            P(UNIT_WIDTH_SHARD),
            P(UNIT_WIDTH_SHARD),
            P("unit"),
        ),
        check_vma=False,
    )
```

profile of v0, /device:TPU:8, one launch (start us, length us, event | category | flops | bytes accessed | tf_op | source)
XLA Modules:
  0.0 163.5 jit_solution(15788300309638621585)
XLA Ops:
  0.6 0.0 copy-start
  0.6 0.0 copy-start.3
  0.7 0.0 copy-start.2
  0.7 0.0 copy-start.1
  0.7 0.8 add_convert_fusion
  1.5 0.6 broadcast_in_dim.2
  2.1 11.9 %all-to-all-start.2 = ((bf16[64,1,56]{2,1,0:T(2,128)(2,1)}), bf16[64,1,56]{2,1,0:T(2,128)(2,1)S(1)}, u32[]{:S(2)}, u32[]{:S(2)}) async-start(bf16[64,1,56]{2,1,0:T(2,128)(2,1)} %broadcast_in_dim.2), calls=%async_computation.2 | async-start | bytes 65536 | tf_op jit(solution)/shard_map/all_to_all | solution.py:26
  14.1 0.0 copy-done
  14.1 3.8 %abs_reduce_fusion = (f32[7168]{0:T(1024)S(1)}, f32[112,7168]{1,0:T(8,128)}) fusion(bf16[112,64]{0,1:T(8,128)(2,1)} %param.12, bf16[64,7168]{1,0:T(8,128)(2,1)S(1)} %copy-done, bf16[112,7168]{1,0:T(8,128)(2,1)} %param.11), kind=kOutput, calls=%fused_computation.5 | convolution fusion | flops 106767360 | bytes 5777408 | tf_op jit(solution)/shard_map/dot_general | solution.py:46
  17.9 0.0 copy-done.3
  17.9 0.0 copy-done.2
  17.9 0.0 copy-done.1
  17.9 2.5 %abs_reduce_fusion.1 = (f32[7168]{0:T(1024)S(1)}, f32[112,7168]{1,0:T(8,128)}) fusion(bf16[112,64]{0,1:T(8,128)(2,1)S(1)} %copy-done.3, bf16[64,7168]{1,0:T(8,128)(2,1)S(1)} %copy-done.2, bf16[112,7168]{1,0:T(8,128)(2,1)S(1)} %copy-done.1), kind=kOutput, calls=%fused_computation.7 | convolution fusion | flops 106767360 | bytes 5777408 | tf_op jit(solution)/shard_map/dot_general | solution.py:43
  20.4 30.4 %all-reduce = (f32[7168]{0:T(1024)S(1)}, f32[7168]{0:T(1024)S(1)}) all-reduce(f32[7168]{0:T(1024)S(1)} %get-tuple-element.14, f32[7168]{0:T(1024)S(1)} %get-tuple-element.16), channel_id=1, replica_groups=mesh['shard_0'=8,'shard_1'=4,'width'=2,'unit'=4] {'shard_0'}, use_global_device_ids=true, to_apply=%region_1.0 | all-reduce | flops 14336 | bytes 114688 | tf_op jit(solution)/shard_map/pmax | solution.py:20
  50.9 17.5 %all-reduce.1 = (f32[7168]{0:T(1024)S(1)}, f32[7168]{0:T(1024)S(1)}) all-reduce(f32[7168]{0:T(1024)S(1)} %get-tuple-element.10, f32[7168]{0:T(1024)S(1)} %get-tuple-element.11), channel_id=1, replica_groups=mesh['shard_0'=8,'shard_1'=4,'width'=2,'unit'=4] {'shard_1'}, use_global_device_ids=true, to_apply=%region_2.0 | all-reduce | flops 14336 | bytes 114688 | tf_op jit(solution)/shard_map/pmax | solution.py:20
  68.4 5.1 %divide_convert_fusion = (bf16[112,7168]{1,0:T(8,128)(2,1)}, bf16[112,7168]{1,0:T(8,128)(2,1)}) fusion(f32[112,7168]{1,0:T(8,128)} %get-tuple-element.17, f32[7168]{0:T(1024)S(1)} %get-tuple-element.13, f32[112,7168]{1,0:T(8,128)} %get-tuple-element.15, f32[7168]{0:T(1024)S(1)} %get-tuple-element.12), kind=kLoop, calls=%fused_computation.4 | loop fusion | flops 3211264 | bytes 9691136 | tf_op jit(solution)/shard_map/convert_element_type | solution.py:55
  73.5 3.9 %all_to_all.32 = bf16[112,32,224]{2,1,0:T(8,128)(2,1)S(1)} reshape(bf16[112,7168]{1,0:T(8,128)(2,1)} %get-tuple-element.19) | data formatting | bytes 3211264 | tf_op jit(solution)/shard_map/all_to_all | solution.py:58
  77.4 2.3 %copy.17 = bf16[112,32,224]{2,0,1:T(8,128)(2,1)} copy(bf16[112,32,224]{2,1,0:T(8,128)(2,1)S(1)} %all_to_all.32) | data formatting | bytes 3211264 | tf_op jit(solution)/shard_map/all_to_all | solution.py:58
  79.6 0.0 all-to-all-done.2
  79.6 5.7 %all-to-all-start = ((bf16[112,32,224]{2,0,1:T(8,128)(2,1)}), bf16[112,32,224]{2,0,1:T(8,128)(2,1)S(1)}, u32[]{:S(2)}, u32[]{:S(2)}) async-start(bf16[112,32,224]{2,0,1:T(8,128)(2,1)} %copy.17), calls=%async_computation | async-start | bytes 3670016 | tf_op jit(solution)/shard_map/all_to_all | solution.py:58
  85.3 4.9 %all_to_all.36 = bf16[112,32,224]{2,1,0:T(8,128)(2,1)} reshape(bf16[112,7168]{1,0:T(8,128)(2,1)} %get-tuple-element.18) | data formatting | bytes 3211264 | tf_op jit(solution)/shard_map/all_to_all | solution.py:59
  90.2 3.7 %copy.18 = bf16[112,32,224]{2,0,1:T(8,128)(2,1)} copy(bf16[112,32,224]{2,1,0:T(8,128)(2,1)} %all_to_all.36) | data formatting | bytes 3211264 | tf_op jit(solution)/shard_map/all_to_all | solution.py:59
  94.0 25.8 %all-to-all-done = bf16[112,32,224]{2,0,1:T(8,128)(2,1)S(1)} async-done(((bf16[112,32,224]{2,0,1:T(8,128)(2,1)}), bf16[112,32,224]{2,0,1:T(8,128)(2,1)S(1)}, u32[]{:S(2)}, u32[]{:S(2)}) %all-to-all-start) | async-done | bytes 1605664 | tf_op jit(solution)/shard_map/all_to_all | solution.py:58
  119.7 5.9 %all-to-all-start.1 = ((bf16[112,32,224]{2,0,1:T(8,128)(2,1)}), bf16[112,32,224]{2,0,1:T(8,128)(2,1)}, u32[]{:S(2)}, u32[]{:S(2)}) async-start(bf16[112,32,224]{2,0,1:T(8,128)(2,1)} %copy.18), calls=%async_computation.1 | async-start | bytes 3670016 | tf_op jit(solution)/shard_map/all_to_all | solution.py:59
  125.6 0.6 dynamic_slice.6
  126.2 0.6 dynamic_slice.7
  126.9 0.1 reduce
  127.0 0.7 reshape.28
  127.7 2.5 %copy.19 = bf16[3584,224]{0,1:T(8,128)(2,1)} copy(bf16[3584,224]{1,0:T(8,128)(2,1)S(1)} %bitcast.10) | data formatting | bytes 3211264
  130.1 29.6 %all-to-all-done.1 = bf16[112,32,224]{2,0,1:T(8,128)(2,1)} async-done(((bf16[112,32,224]{2,0,1:T(8,128)(2,1)}), bf16[112,32,224]{2,0,1:T(8,128)(2,1)}, u32[]{:S(2)}, u32[]{:S(2)}) %all-to-all-start.1) | async-done | bytes 1605664 | tf_op jit(solution)/shard_map/all_to_all | solution.py:59
  159.7 3.8 %copy.20 = bf16[3584,224]{0,1:T(8,128)(2,1)} copy(bf16[3584,224]{1,0:T(8,128)(2,1)} %bitcast.3) | data formatting | bytes 3211264
Async XLA Ops:
  0.6 13.5 %copy-start = (bf16[64,7168]{1,0:T(8,128)(2,1)S(1)}, bf16[64,7168]{1,0:T(8,128)(2,1)}, u32[]{:S(2)}) copy-start(bf16[64,7168]{1,0:T(8,128)(2,1)} %param.13) | copy-start | bytes 2752516
  0.6 17.3 %copy-start.3 = (bf16[112,64]{0,1:T(8,128)(2,1)S(1)}, bf16[112,64]{0,1:T(8,128)(2,1)}, u32[]{:S(2)}) copy-start(bf16[112,64]{0,1:T(8,128)(2,1)} %param.9) | copy-start | bytes 43012
  0.7 17.3 %copy-start.2 = (bf16[64,7168]{1,0:T(8,128)(2,1)S(1)}, bf16[64,7168]{1,0:T(8,128)(2,1)}, u32[]{:S(2)}) copy-start(bf16[64,7168]{1,0:T(8,128)(2,1)} %param.10) | copy-start | bytes 2752516
  0.7 17.3 %copy-start.1 = (bf16[112,7168]{1,0:T(8,128)(2,1)S(1)}, bf16[112,7168]{1,0:T(8,128)(2,1)}, u32[]{:S(2)}) copy-start(bf16[112,7168]{1,0:T(8,128)(2,1)} %param.8) | copy-start | bytes 4816900
  2.1 77.5 %all-to-all-start.2 = ((bf16[64,1,56]{2,1,0:T(2,128)(2,1)}), bf16[64,1,56]{2,1,0:T(2,128)(2,1)S(1)}, u32[]{:S(2)}, u32[]{:S(2)}) async-start(bf16[64,1,56]{2,1,0:T(2,128)(2,1)} %broadcast_in_dim.2), calls=%async_computation.2 | async-start | bytes 65536 | tf_op jit(solution)/shard_map/all_to_all | solution.py:26
  79.6 40.1 %all-to-all-start = ((bf16[112,32,224]{2,0,1:T(8,128)(2,1)}), bf16[112,32,224]{2,0,1:T(8,128)(2,1)S(1)}, u32[]{:S(2)}, u32[]{:S(2)}) async-start(bf16[112,32,224]{2,0,1:T(8,128)(2,1)} %copy.17), calls=%async_computation | async-start | bytes 3670016 | tf_op jit(solution)/shard_map/all_to_all | solution.py:58
  119.7 40.0 %all-to-all-start.1 = ((bf16[112,32,224]{2,0,1:T(8,128)(2,1)}), bf16[112,32,224]{2,0,1:T(8,128)(2,1)}, u32[]{:S(2)}, u32[]{:S(2)}) async-start(bf16[112,32,224]{2,0,1:T(8,128)(2,1)} %copy.18), calls=%async_computation.1 | async-start | bytes 3670016 | tf_op jit(solution)/shard_map/all_to_all | solution.py:59
where the time goes:
time: 164 us; the launch traced here: 163 us
  waiting for transfers between devices  55.4 us (34%)
  blocking collectives  47.9 us (29%)
  local copies, waits for them, and re-layouts  23.7 us (14%)
  starting transfers between devices  23.5 us (14%)
  matrix products  6.31 us (4%)
  other arithmetic  6.03 us (4%)
    pmax x2, blocking collectives, one_axis_at_a_time(): array = lax.pmax(array, axis)  47.9 us
    all_to_all x1, waiting for transfers between devices, local(): lax.all_to_all(narrow_up, SHARD, split_axis=1, concat_axis=0, tiled=True)  29.6 us
    all_to_all x1, waiting for transfers between devices, local(): lax.all_to_all(narrow_gate, SHARD, split_axis=1, concat_axis=0, tiled=True)  25.8 us
    all_to_all x1, starting transfers between devices, from_everyone(): lax.all_to_all(jnp.broadcast_to(array[None], (count, *array.shape)), axis...  11.9 us
    all_to_all x2, local copies, waits for them, and re-layouts, local(): lax.all_to_all(narrow_up, SHARD, split_axis=1, concat_axis=0, tiled=True)  8.65 us
    unnamed x10, local copies, waits for them, and re-layouts  6.25 us
    all_to_all x2, local copies, waits for them, and re-layouts, local(): lax.all_to_all(narrow_gate, SHARD, split_axis=1, concat_axis=0, tiled=True)  6.15 us
    all_to_all x1, starting transfers between devices, local(): lax.all_to_all(narrow_up, SHARD, split_axis=1, concat_axis=0, tiled=True)  5.86 us
  transfers between devices with their start and end apart: 3, of which 2 were waited for; matrix products, arithmetic and copies ran while one was open for 13% of the time, Pallas kernels for 0%

commit v1 on v0

v1 whole, which is shorter than its diff:
```python
import jax
import jax.numpy as jnp
from jax import lax
from jax.experimental import pallas as pl
from jax.experimental.pallas import tpu as pltpu
from jax.sharding import PartitionSpec as P

MESH = pl.DeviceIdType.MESH
NZ, NX = 8, 4
ROWS = 112
COLS = 224
RANK = 64
PLANE = NX * COLS
LANES = 128
NEAR = 2 * LANES
WIDE = 3 * LANES
TOTAL = NZ * NX * ROWS
NORM = 56
SLOT = 4 * LANES
HALF = SLOT - NX * ROWS
mix_rate = 0.5


def tile_of(x):
    return (7 * x) // 4


ORDER = (1, 7, 2, 6, 3, 5, 4)
EARLY = ((1, 1), (7, 1))
PIECES = [
    (dz, a, 0, ROWS)
    for dz, a in (
        (1, 0), (7, 0), (4, 0), (2, 0), (6, 0), (3, 0), (5, 0), (4, 1), (3, 1), (5, 1), (2, 1), (6, 1),
    )
]
OWN = [(0, a, 0, ROWS) for a in range(2)]
ALL = OWN + PIECES


def exchange_kernel(
    w_gate,
    low_gate,
    high_gate,
    w_up,
    low_up,
    high_up,
    norm_train,
    norm_step,
    fresh_gate,
    fresh_up,
    peak,
    norm_out,
    zbuf,
    pack,
    xbuf,
    early,
    earlypack,
    earlyrow,
    lowown,
    lowbuf,
    lowrows,
    normbuf,
    hbuf,
    hturn,
    pick,
    hcols,
    norm_abs,
    norm_acc,
    local_sem,
    zs,
    zr,
    xs,
    xr,
    lzs,
    lzr,
    lxs,
    lxr,
    nzs,
    nzr,
    nxs,
    nxr,
    ds,
    dr,
    exs,
    exr,
    ezs,
    ezr,
):
    place = lax.axis_index("shard")
    core = lax.axis_index("width")
    z, x = place // NX, lax.rem(place, NX)
    weights = (w_gate, w_up)
    fresh = (fresh_gate, fresh_up)

    def at(dz, dx):
        return lax.rem(z + dz, NZ) * NX + lax.rem(x + dx, NX)

    def zpeer(dz):
        return {"shard": at(dz, 0)}

    def xpeer(dx):
        return {"shard": at(0, dx)}

    partner = {"width": 1 - core}

    def remote(source, target, send, receive, peer):
        return pltpu.make_async_remote_copy(
            src_ref=source,
            dst_ref=target,
            send_sem=send,
            recv_sem=receive,
            device_id=peer,
            device_id_type=MESH,
        )

    barrier = pltpu.get_barrier_semaphore()
    for dz in range(1, NZ):
        pl.semaphore_signal(barrier, inc=1, device_id=zpeer(dz), device_id_type=MESH)
    for dx in range(1, NX):
        pl.semaphore_signal(barrier, inc=1, device_id=xpeer(dx), device_id_type=MESH)
    pl.semaphore_signal(barrier, inc=1, device_id=partner, device_id_type=MESH)

    first = tile_of(x)
    start = pl.multiple_of(z * PLANE, LANES)
    hstart = pl.multiple_of(z * PLANE + first * LANES, LANES)
    offset = lax.rem(96 * x, LANES)
    wide = jnp.logical_or(x == 1, x == 2)

    def own_block(a):
        return pltpu.make_async_copy(
            weights[a].at[:, pl.ds(start, PLANE)], zbuf.at[0, a], local_sem.at[a]
        )

    def early_block(k):
        dz, a = EARLY[k]
        column = pl.multiple_of(lax.rem(z + dz, NZ) * PLANE, LANES)
        return pltpu.make_async_copy(
            weights[a].at[:, pl.ds(column, PLANE)], early.at[k], local_sem.at[9 + k]
        )

    highs = (high_gate, high_up)

    def own_high(a):
        return pltpu.make_async_copy(
            highs[a].at[:, pl.ds(hstart, NEAR)],
            hbuf.at[a, :, pl.ds(0, NEAR)],
            local_sem.at[2 + a],
        )

    def own_high_rest(a):
        rest = pl.multiple_of(hstart + NEAR, LANES)
        return pltpu.make_async_copy(
            highs[a].at[:, pl.ds(rest, LANES)],
            hbuf.at[a, :, pl.ds(NEAR, LANES)],
            local_sem.at[4 + a],
        )

    lows = (low_gate, low_up)

    def own_low(a):
        return pltpu.make_async_copy(lows[a], lowown, local_sem.at[6])

    norms = (norm_train, norm_step)

    def own_norm(k):
        return pltpu.make_async_copy(norms[k], normbuf.at[0, 0, 0, k], local_sem.at[7 + k])

    for a in range(2):

        @pl.when(core == a)
        def _():
            own_low(a).start()

    for a in range(2):
        own_block(a).start()
    for k in range(len(EARLY)):
        early_block(k).start()
    for a in range(2):
        own_high(a).start()

        @pl.when(wide)
        def _():
            own_high_rest(a).start()

        own_norm(a).start()

    lowbuf[0, 0, 0] = jnp.zeros((RANK, LANES), jnp.bfloat16)
    own_low(0).wait()
    lowbuf[0, 0, 0, :, :ROWS] = lowown[...]

    pl.semaphore_wait(barrier, NZ - 1 + NX - 1 + 1)

    def low_z(dz):
        return remote(lowbuf.at[0, 0, 0], lowbuf.at[0, 0, dz], lzs.at[dz], lzr.at[dz], zpeer(dz))

    def norm_z(k, dz):
        return remote(
            norms[k], normbuf.at[0, 0, dz, k], nzs.at[dz, k], nzr.at[dz, k], zpeer(dz)
        )

    def block_z(i):
        dz, a, row, count = PIECES[i]
        column = pl.multiple_of(lax.rem(z + dz, NZ) * PLANE, LANES)
        return remote(
            weights[a].at[pl.ds(row, count), pl.ds(column, PLANE)],
            zbuf.at[dz, a, pl.ds(row, count)],
            zs.at[i],
            zr.at[i],
            zpeer(dz),
        )

    for dz in ORDER:
        low_z(dz).start()
    for dz in ORDER:
        for k in range(2):
            norm_z(k, dz).start()
    for i in range(len(PIECES)):
        block_z(i).start()

    def slot_row(dz, there):
        plane = lax.rem(z + NZ - dz, NZ)
        return pl.multiple_of(there * ROWS + lax.rem(plane, 2) * HALF, 16)

    def block_x(i, dx):
        dz, a, row, count = ALL[i]
        there = lax.rem(x + dx, NX)
        target = pl.multiple_of(slot_row(dz, x) + row, 16)
        return remote(
            pack.at[dz, a, there, pl.ds(row, count)],
            xbuf.at[a, dz, pl.ds(target, count)],
            xs.at[i, dx],
            xr.at[i, dx],
            xpeer(dx),
        )

    def columns_for(source, rows, there):
        begin, shift = divmod(there * COLS, LANES)
        width = min(WIDE, PLANE - begin * LANES)
        if not shift:
            return source[rows, pl.ds(0, NEAR)]
        taken = source[rows, pl.ds(begin * LANES, width)].astype(jnp.float32)
        return pltpu.roll(taken, width - shift, 1)[:, :NEAR].astype(jnp.bfloat16)

    def early_x(k, dx):
        there = lax.rem(x + dx, NX)
        return remote(
            earlypack.at[k, there],
            earlyrow.at[k, pl.ds(pl.multiple_of(x * ROWS, 16), ROWS)],
            exs.at[k, dx],
            exr.at[k, dx],
            xpeer(dx),
        )

    def early_z(k):
        dz, a = EARLY[k]
        row = pl.multiple_of(lax.rem(z, 2) * HALF, HALF)
        return remote(
            earlyrow.at[k], xbuf.at[a, dz, pl.ds(row, NX * ROWS)], ezs.at[k], ezr.at[k], zpeer(dz)
        )

    def early_start(k):
        early_block(k).wait()
        for there in range(NX):
            moved = columns_for(early.at[k], pl.ds(0, ROWS), there)
            earlypack[k, there] = moved

            @pl.when(x == there)
            def _():
                earlyrow[k, there * ROWS : (there + 1) * ROWS] = moved

        for dx in (1, 3, 2):
            early_x(k, dx).start()

    def early_on(k):
        for dx in (1, 3, 2):
            early_x(k, dx).wait_recv()
        early_z(k).start()

    def forward(i):
        dz, a, row, count = ALL[i]
        target = pl.multiple_of(slot_row(dz, x) + row, 16)
        rows = pl.ds(row, count)
        for there in range(NX):
            moved = columns_for(zbuf.at[dz, a], rows, there)
            pack[dz, a, there, rows] = moved

            @pl.when(x == there)
            def _():
                xbuf[a, dz, pl.ds(target, count)] = moved

        for dx in (1, 3, 2):
            block_x(i, dx).start()

    def low_x(dx):
        return remote(lowbuf.at[0, 0], lowbuf.at[0, dx], lxs.at[dx], lxr.at[dx], xpeer(dx))

    def norm_x(dx):
        return remote(normbuf.at[0, 0], normbuf.at[0, dx], nxs.at[dx], nxr.at[dx], xpeer(dx))

    def low_core():
        return remote(lowbuf.at[0], lowbuf.at[1], ds.at[0], dr.at[0], partner)

    def norm_core():
        return remote(normbuf.at[0], normbuf.at[1], ds.at[1], dr.at[1], partner)

    for a in range(2):
        for dz in range(NZ):
            odd = lax.rem(z + NZ - dz, NZ)
            spare = pl.ds(pl.multiple_of((1 - lax.rem(odd, 2)) * NX * ROWS, HALF), HALF)
            xbuf[a, dz, spare] = jnp.zeros((HALF, NEAR), jnp.bfloat16)
            lowrows[a, dz, spare] = jnp.zeros((HALF, RANK), jnp.bfloat16)

    for k in range(len(EARLY)):
        early_start(k)
    for a in range(2):
        own_block(a).wait()
        forward(a)
    for a in range(2):
        own_norm(a).wait()
        own_high(a).wait()

        @pl.when(wide)
        def _():
            own_high_rest(a).wait()

        @pl.when(jnp.logical_not(wide))
        def _():
            hbuf[a, :, NEAR:] = jnp.zeros((RANK, LANES), jnp.bfloat16)

    low = pl.multiple_of(offset, 32)
    row_of = lax.broadcasted_iota(jnp.int32, (COLS, NEAR), 0)
    lane_of = lax.broadcasted_iota(jnp.int32, (COLS, NEAR), 1)
    pick[...] = jnp.where(lane_of == row_of, 1.0, 0.0).astype(jnp.bfloat16)
    for a in range(2):
        hturn[...] = hbuf[a].astype(jnp.float32).T
        hcols[a] = hturn[pl.ds(low, COLS), :].astype(jnp.bfloat16)
        peak[a] = jnp.zeros((COLS, LANES), jnp.float32)

    def turn_low():
        for a in range(2):
            held = jnp.where(core == a, 0, 1)

            @pl.loop(0, NX)
            def _(dx):
                there = lax.rem(x + NX - dx, NX)

                @pl.loop(0, NZ)
                def _(dz):
                    block = lowbuf[held, dx, dz].astype(jnp.float32).T[:ROWS]
                    lowrows[a, dz, pl.ds(slot_row(dz, there), ROWS)] = block.astype(jnp.bfloat16)

    def merge(a, dz):
        if (dz, a) in EARLY:
            early_z(EARLY.index((dz, a))).wait_recv()
        for i, piece in enumerate(ALL):
            if piece[:2] == (dz, a):
                for dx in (1, 3, 2):
                    block_x(i, dx).wait_recv()
        plane = lax.rem(z + NZ - dz, NZ) * SLOT
        turned = (((1,), (1,)), ((), ()))
        for half in range(0, SLOT, NEAR):
            base = lax.dot_general(
                pick[...],
                xbuf[a, dz, half : half + NEAR, :],
                turned,
                preferred_element_type=jnp.float32,
            )
            product = lax.dot_general(
                hcols[a],
                lowrows[a, dz, half : half + NEAR, :],
                turned,
                preferred_element_type=jnp.float32,
            )
            value = base + mix_rate * product
            fresh[a][:, pl.ds(pl.multiple_of(plane + half, NEAR), NEAR)] = value
            size = jnp.abs(value)
            peak[a] = jnp.maximum(peak[a], jnp.maximum(size[:, :LANES], size[:, LANES:]))

    def gather_norm():
        @pl.loop(0, NX)
        def _(dx):
            @pl.loop(0, NZ)
            def _(dz):
                who = lax.rem(z + NZ - dz, NZ) * NX + lax.rem(x + NX - dx, NX)
                for c in range(2):
                    side = core if c == 0 else 1 - core
                    total = normbuf[c, dx, dz, 0] + normbuf[c, dx, dz, 1]
                    norm_abs[pl.ds(who * 2 + side, 1), pl.ds(0, NORM)] = total

        rows = [jnp.zeros((4, LANES), jnp.float32) for _ in range(7)]
        lane = lax.broadcasted_iota(jnp.int32, (4, LANES), 1)
        for j in range(16):
            begin = NORM * j
            row, shift = begin // LANES, begin % LANES
            taken = norm_abs[pl.ds(j, 4, stride=16), :]
            moved = pltpu.roll(taken, shift, 1) if shift else taken
            end = shift + NORM
            inside = jnp.logical_and(lane >= shift, lane < end)
            rows[row] = jnp.where(inside, moved, rows[row])
            if end > LANES:
                rows[row + 1] = jnp.where(lane < end - LANES, moved, rows[row + 1])
        for q in range(7):
            norm_acc[pl.ds(q, 4, stride=7), :] = rows[q]
        norm_out[...] = norm_acc[...].astype(jnp.bfloat16)

    blocks = [piece[:2] for piece in ALL] + list(EARLY)
    done = 0
    for i, (dz, a, row, count) in enumerate(PIECES):
        block_z(i).wait_recv()
        forward(len(OWN) + i)
        if i < len(EARLY):
            early_on(i)
        if i == 2:
            for far in ORDER:
                low_z(far).wait_recv()
            for dx in (1, 3, 2):
                low_x(dx).start()
        if i == 4:
            for dx in (1, 3, 2):
                low_x(dx).wait_recv()
            low_core().start()
        if i == 6:
            low_core().wait_recv()
            turn_low()
        if i == 4:
            for far in ORDER:
                for k in range(2):
                    norm_z(k, far).wait_recv()
            for dx in (1, 3, 2):
                norm_x(dx).start()
        if i == 6:
            for dx in (1, 3, 2):
                norm_x(dx).wait_recv()
            norm_core().start()
        if i == 8:
            norm_core().wait_recv()
            gather_norm()
        if i >= 6:
            for _ in range(3):
                if blocks[done] != (dz, a):
                    merge(blocks[done][1], blocks[done][0])
                    done += 1
    while done < len(blocks):
        merge(blocks[done][1], blocks[done][0])
        done += 1

    for k in range(len(EARLY)):
        early_z(k).wait_send()
        for dx in (1, 3, 2):
            early_x(k, dx).wait_send()
    for i in range(len(PIECES)):
        block_z(i).wait_send()
    for dz in ORDER:
        low_z(dz).wait_send()
        for k in range(2):
            norm_z(k, dz).wait_send()
    for dx in (1, 3, 2):
        low_x(dx).wait_send()
        norm_x(dx).wait_send()
        for i in range(len(ALL)):
            block_x(i, dx).wait_send()
    low_core().wait_send()
    norm_core().wait_send()


CHUNK = 32


def finish_kernel(
    fresh_gate,
    fresh_up,
    peak,
    norm,
    serve_gate,
    serve_up,
    column_gate,
    column_up,
    serve_norm,
    held,
    sem,
):
    targets = (serve_gate, serve_up)
    columns = (column_gate, column_up)
    for a, source in enumerate((fresh_gate, fresh_up)):

        @pl.loop(0, COLS // CHUNK)
        def _(i):
            rows = pl.ds(pl.multiple_of(i * CHUNK, CHUNK), CHUNK)
            scale = 1.0 / jnp.max(peak[a, rows, :], axis=1, keepdims=True)
            for pair in range(NZ // 2):
                even = source[rows, pl.ds(2 * pair * SLOT, SLOT)]
                odd = source[rows, pl.ds((2 * pair + 1) * SLOT, SLOT)]
                begin = 2 * pair * NX * ROWS
                parts = (even[:, :WIDE], even[:, WIDE:] + odd[:, :LANES], odd[:, LANES:])
                for part in parts:
                    width = part.shape[1]
                    held[a, rows, pl.ds(begin, width)] = (part * scale).astype(jnp.bfloat16)
                    begin += width
            pltpu.make_async_copy(held.at[a, rows], targets[a].at[rows], sem.at[a, i]).start()

    for a in range(2):
        columns[a][...] = jnp.max(peak[a].T, axis=0, keepdims=True)
    serve_norm[...] = norm[...]
    for a in range(2):

        @pl.loop(0, COLS // CHUNK)
        def _(i):
            rows = pl.ds(pl.multiple_of(i * CHUNK, CHUNK), CHUNK)
            pltpu.make_async_copy(held.at[a, rows], targets[a].at[rows], sem.at[a, i]).wait()


def local(w_gate, low_gate, high_gate, w_up, low_up, high_up, norm_train, norm_step):
    anywhere = pl.BlockSpec(memory_space=pl.ANY)
    vmem = pl.BlockSpec(memory_space=pltpu.VMEM)
    dma = pltpu.SemaphoreType.DMA
    def outside(v):
        return pltpu.with_memory_space_constraint(v, pltpu.HBM)

    fresh_gate, fresh_up, peak, norm = pl.pallas_call(
        exchange_kernel,
        name="exchange",
        out_shape=(
            pltpu.VMEM((COLS, NZ * SLOT), jnp.float32),
            pltpu.VMEM((COLS, NZ * SLOT), jnp.float32),
            pltpu.VMEM((2, COLS, LANES), jnp.float32),
            pltpu.VMEM((28, LANES), jnp.bfloat16),
        ),
        in_specs=[anywhere] * 8,
        out_specs=(vmem,) * 4,
        scratch_shapes=[
            pltpu.VMEM((NZ, 2, ROWS, PLANE), jnp.bfloat16),
            pltpu.VMEM((NZ, 2, NX, ROWS, NEAR), jnp.bfloat16),
            pltpu.VMEM((2, NZ, SLOT, NEAR), jnp.bfloat16),
            pltpu.VMEM((len(EARLY), ROWS, PLANE), jnp.bfloat16),
            pltpu.VMEM((len(EARLY), NX, ROWS, NEAR), jnp.bfloat16),
            pltpu.VMEM((len(EARLY), NX * ROWS, NEAR), jnp.bfloat16),
            pltpu.VMEM((RANK, ROWS), jnp.bfloat16),
            pltpu.VMEM((2, NX, NZ, RANK, LANES), jnp.bfloat16),
            pltpu.VMEM((2, NZ, SLOT, RANK), jnp.bfloat16),
            pltpu.VMEM((2, NX, NZ, 2, 1, NORM), jnp.float32),
            pltpu.VMEM((2, RANK, WIDE), jnp.bfloat16),
            pltpu.VMEM((WIDE, RANK), jnp.float32),
            pltpu.VMEM((COLS, NEAR), jnp.bfloat16),
            pltpu.VMEM((2, COLS, RANK), jnp.bfloat16),
            pltpu.VMEM((64, LANES), jnp.float32),
            pltpu.VMEM((28, LANES), jnp.float32),
            dma((9 + len(EARLY),)),
            dma((len(PIECES),)),
            dma((len(PIECES),)),
            dma((len(ALL), NX)),
            dma((len(ALL), NX)),
            dma((NZ,)),
            dma((NZ,)),
            dma((NX,)),
            dma((NX,)),
            dma((NZ, 2)),
            dma((NZ, 2)),
            dma((NX,)),
            dma((NX,)),
            dma((2,)),
            dma((2,)),
            dma((len(EARLY), NX)),
            dma((len(EARLY), NX)),
            dma((len(EARLY),)),
            dma((len(EARLY),)),
        ],
        compiler_params=pltpu.CompilerParams(
            collective_id=0, has_side_effects=True, vmem_limit_bytes=32 * 1024 * 1024
        ),
    )(
        outside(w_gate),
        outside(low_gate.T),
        outside(high_gate),
        outside(w_up),
        outside(low_up.T),
        outside(high_up),
        outside(norm_train.reshape(1, NORM)),
        outside(norm_step.reshape(1, NORM)),
    )
    inside = [
        pltpu.with_memory_space_constraint(v, pltpu.VMEM)
        for v in (fresh_gate, fresh_up, peak, norm)
    ]
    serve_gate, serve_up, column_gate, column_up, serve_norm = pl.pallas_call(
        finish_kernel,
        name="finish",
        out_shape=(
            jax.ShapeDtypeStruct((COLS, TOTAL), jnp.bfloat16),
            jax.ShapeDtypeStruct((COLS, TOTAL), jnp.bfloat16),
            jax.ShapeDtypeStruct((1, COLS), jnp.float32),
            jax.ShapeDtypeStruct((1, COLS), jnp.float32),
            jax.ShapeDtypeStruct((28, LANES), jnp.bfloat16),
        ),
        in_specs=[vmem] * 4,
        out_specs=(anywhere, anywhere, vmem, vmem, vmem),
        scratch_shapes=[
            pltpu.VMEM((2, COLS, TOTAL), jnp.bfloat16),
            dma((2, COLS // CHUNK)),
        ],
        compiler_params=pltpu.CompilerParams(vmem_limit_bytes=16 * 1024 * 1024),
    )(*inside)
    return (
        serve_gate.T,
        serve_up.T,
        column_gate.reshape(COLS),
        column_up.reshape(COLS),
        serve_norm.reshape(28 * LANES),
    )


def solution(mesh):
    rows = ("unit", "shard")
    return jax.shard_map(
        local,
        mesh=mesh,
        in_specs=(
            P(rows, "width"),
            P(rows, None),
            P("unit", "width"),
            P(rows, "width"),
            P(rows, None),
            P("unit", "width"),
            P(("unit", "shard", "width")),
            P(("unit", "shard", "width")),
        ),
        out_specs=(
            P("unit", ("width", "shard")),
            P("unit", ("width", "shard")),
            P(("unit", "width", "shard")),
            P(("unit", "width", "shard")),
            P("unit"),
        ),
        check_vma=False,
    )
```

time: 164 us -> 91.4 us (0.56)
  Pallas kernels: 0 us -> 90.5 us
  waiting for transfers between devices: 55.4 us -> 0 us
  blocking collectives: 47.9 us -> 0 us
  local copies, waits for them, and re-layouts: 23.7 us -> 0 us
  starting transfers between devices: 23.5 us -> 0 us
  matrix products: 6.31 us -> 0 us
  other arithmetic: 6.03 us -> 0 us
    pallas_call x0 -> x2, Pallas kernels: none -> 90.5 us  [the longest x1 87.5 us: local(): pl.pallas_call(exchange_kernel, name='exchange', out_shape=(pltpu.VMEM((C...]
    all_to_all x3 -> x0, waiting for transfers between devices: 55.4 us -> none  [the longest x1 29.6 us: local(): lax.all_to_all(narrow_up, SHARD, split_axis=1, concat_axis=0, tiled=True)]
    pmax x2 -> x0, blocking collectives: 47.9 us -> none  [one_axis_at_a_time(): array = lax.pmax(array, axis)]
    all_to_all x3 -> x0, starting transfers between devices: 23.5 us -> none  [the longest x1 11.9 us: from_everyone(): lax.all_to_all(jnp.broadcast_to(array[None], (count, *array.shape)), axis...]
    all_to_all x4 -> x0, local copies, waits for them, and re-layouts: 14.8 us -> none  [the longest x2 8.65 us: local(): lax.all_to_all(narrow_up, SHARD, split_axis=1, concat_axis=0, tiled=True)]
    dot_general x2 -> x0, matrix products: 6.31 us -> none  [the longest x1 3.84 us: local(): jnp.dot(low_up, high_up, preferred_element_type=jnp.float32)]
    unnamed x10 -> x0, local copies, waits for them, and re-layouts: 6.25 us -> none
    convert_element_type x2 -> x0, other arithmetic: 5.93 us -> none  [the longest x1 5.1 us: local(): (fresh_up / column_up).astype(jnp.bfloat16)]
  transfers between devices with their start and end apart: 3 -> 0, of which waited for: 2 -> 0; matrix products, arithmetic and copies ran while one was open for 13% -> 0% of each run, Pallas kernels for 0% -> 0%
where the time goes in v1:
time: 91.4 us; the launch traced here: 91.2 us
  Pallas kernels  90.5 us (99%)
    pallas_call x1, Pallas kernels, local(): pl.pallas_call(exchange_kernel, name='exchange', out_shape=(pltpu.VMEM((C...  87.5 us
    pallas_call x1, Pallas kernels, local(): pl.pallas_call(finish_kernel, name='finish', out_shape=(jax.ShapeDtypeStr...  3.01 us

profile of v1, /device:TPU:8, one launch (start us, length us, event | category | flops | bytes accessed | tf_op | source)
XLA Modules:
  0.0 91.2 jit_solution(14262490676253490644)
XLA Ops:
  0.6 87.5 %exchange.1 = (f32[224,4096]{1,0:T(8,128)S(1)}, f32[224,4096]{1,0:T(8,128)S(1)}, f32[2,224,128]{2,1,0:T(8,128)S(1)}, bf16[28,128]{1,0:T(8,128)(2,1)S(1)}) custom-call(bf16[112,7168]{1,0:T(8,128)(2,1)} %w_gate.1, bf16[64,112]{1,0:T(8,128)(2,1)} %bitcast.9, bf16[64,7168]{1,0:T(8,128)(2,1)} %high_gate.1, bf16[112,7168]{1,0:T(8,128)(2,1)} %w_up.1, ...), custom_call_target="tpu_custom_call" | custom-call | tf_op jit(solution)/shard_map/exchange/pallas_call | solution.py:519
  88.2 3.0 %finish.1 = (bf16[224,3584]{1,0:T(8,128)(2,1)}, bf16[224,3584]{1,0:T(8,128)(2,1)}, f32[1,224]{1,0:T(1,128)}, f32[1,224]{1,0:T(1,128)}, bf16[28,128]{1,0:T(8,128)(2,1)}) custom-call(f32[224,4096]{1,0:T(8,128)S(1)} %get-tuple-element.14.fresh_gate, f32[224,4096]{1,0:T(8,128)S(1)} %get-tuple-element.15.fresh_up, f32[2,224,128]{2,1,0:T(8,128)S(1)} %get-tuple-element.16.peak, ...), custom_call_target="tpu_custom_call" | custom-call | tf_op jit(solution)/shard_map/finish/pallas_call | solution.py:584
